TPU v7x, 32 devices: a whole 2x2x4 slice. The times are simulated.
32 devices in a mesh: shard: 8 (over z, core), rep: 4 (over y, x).
Axes of the slice: x: 2, y: 2, z: 4, core: 2. Of those that a mesh axis runs over, the one named last changes fastest.
Arguments:
- tokens: bfloat16 [12288, 5120], P(('shard', 'rep')), may hold values from -700 to 700
- norm_gain: float32 [5120], replicated, may hold values from 0.1 to 1.9
- key_bias: float32 [1024], replicated, may hold values from -4 to 4
- key_weight: bfloat16 [8192, 1024], P('shard'), may hold values from -0.078125 to 0.078125
- cotangent: bfloat16 [12288, 1024], P(('shard', 'rep')), may hold values from -40 to 40
- block_slot: int32 [40], replicated, may hold values from 0 to 63, as said below
Outputs:
- projected: bfloat16 [12288, 1024], P(('shard', 'rep'))
- token_grad: bfloat16 [12288, 5120], P(('shard', 'rep'))
- weight_grad: float32 [8192, 1024], P('shard')
- gain_grad: float32 [5120], replicated
- bias_grad: float32 [1024], replicated
Inputs may be any that keep to these rules, and one draw needn't show every extreme that they name: Entries are distinct; block b lies on the device of shard with index block_slot[b] // 8, at its local slot block_slot[b] % 8; in every draw some device holds 8 blocks.
All inputs are finite; a program needn't handle non-finite values.
Results may differ from a plain program's by a relative error of at most 0.013.
Values may be sent and summed in bfloat16 or wider, within the bound.
A program may use at most 128 MiB of HBM per device.

v0:
```python
import jax
import jax.numpy as jnp
from jax import lax
from jax.sharding import PartitionSpec as P

BLK = 128
EPS = 1e-06


def normalize(tokens, norm_gain):
    values = tokens.astype(jnp.float32)
    inv_rms = lax.rsqrt(jnp.mean(values * values, axis=-1, keepdims=True) + EPS)
    normed = (values * inv_rms * norm_gain).astype(jnp.bfloat16)
    return (values, inv_rms, normed)


def token_backward(values, inv_rms, grad_normed, norm_gain):
    scaled = grad_normed * norm_gain
    inner = jnp.mean(scaled * values, axis=-1, keepdims=True)
    return (inv_rms * (scaled - values * inv_rms * inv_rms * inner)).astype(jnp.bfloat16)


def local(tokens, norm_gain, key_bias, key_weight, cotangent, block_slot):
    values, inv_rms, normed = normalize(tokens, norm_gain)
    row_count = tokens.shape[0]
    width = tokens.shape[1]
    local_rows = key_weight.shape[0]
    shard_count = lax.axis_size("shard")
    replicas = lax.axis_size("rep")
    slot_total = shard_count * local_rows // BLK
    block_count = width // BLK
    block_of_slot = (
        jnp.full((slot_total,), -1, jnp.int32)
        .at[block_slot]
        .set(jnp.arange(block_count, dtype=jnp.int32))
    )
    present = block_of_slot >= 0
    normed_blocks = normed.reshape(row_count, block_count, BLK)
    normed_slots = jnp.take(normed_blocks, jnp.maximum(block_of_slot, 0), axis=1)
    normed_slots = jnp.where(present[None, :, None], normed_slots, jnp.zeros((), jnp.bfloat16))
    normed_slots = normed_slots.reshape(row_count, slot_total * BLK)
    piece = lax.all_gather(key_weight, "shard", axis=0, tiled=True)
    columns = normed_slots
    forward_sum = jnp.dot(columns, piece, preferred_element_type=jnp.float32)
    backward_part = lax.dot_general(
        cotangent, piece, (((1,), (1,)), ((), ())), preferred_element_type=jnp.float32
    )
    projected = (forward_sum + key_bias).astype(jnp.bfloat16)
    grad_normed = jnp.take(backward_part.reshape(row_count, slot_total, BLK), block_slot, axis=1)
    grad_normed = grad_normed.reshape(row_count, width)
    token_grad = token_backward(values, inv_rms, grad_normed, norm_gain)
    grad_scale = float(row_count * shard_count * replicas) ** (-0.5)
    columns = normed_slots
    group_sum = lax.psum_scatter(
        (
            lax.dot_general(
                columns, cotangent, (((0,), (0,)), ((), ())), preferred_element_type=jnp.float32
            )
            * grad_scale
        ).astype(jnp.bfloat16),
        "shard",
        scatter_dimension=0,
        tiled=True,
    ).astype(jnp.float32)
    gain_part = jnp.sum(grad_normed * values * inv_rms, axis=0) * grad_scale
    bias_part = jnp.sum(cotangent.astype(jnp.float32), axis=0) * grad_scale
    weight_grad = lax.psum(group_sum, "rep")
    gain_grad, bias_grad = lax.psum((gain_part, bias_part), ("shard", "rep"))
    return (projected, token_grad, weight_grad, gain_grad, bias_grad)


def solution(mesh):
    return jax.shard_map(
        local,
        mesh=mesh,
        in_specs=(
            P(("shard", "rep"), None),
            P(),
            P(),
            P("shard", None),
            P(("shard", "rep"), None),
            P(),
        ),
        out_specs=(
            P(("shard", "rep"), None),
            P(("shard", "rep"), None),
            P("shard", None),
            P(),
            P(),
        ),
        check_vma=False,
    )
```

profile of v0, /device:TPU:16, one launch (start us, length us, event | category | flops | bytes accessed | tf_op | source)
XLA Modules:
  0.0 578.5 jit_solution(7815864115164983269)
XLA Ops:
  7.2 0.0 copy-start.6
  7.2 0.0 copy-start.3
  7.2 0.0 all-gather.2.cloned.1.call-start
  7.2 0.7 all-gather.2.cloned.1.call-update
  7.9 0.0 reduce-scatter.2.cloned.1.call-start
  8.0 6.3 %copy.12 = bf16[384,5120]{0,1:T(8,128)(2,1)} copy(bf16[384,5120]{1,0:T(8,128)(2,1)} %param.6) | data formatting | bytes 7864320 | tf_op args[0]
  14.2 0.0 copy-done.6
  14.2 0.7 scatter_custom_fusion
  15.0 3.0 fusion.7
  18.1 0.1 broadcast_bitcast_fusion.2
  18.1 0.1 broadcast_bitcast_fusion
  18.2 141.7 %all-gather.2.cloned.1.call-done = bf16[8192,1024]{1,0:T(8,128)(2,1)} async-done(((bf16[1024,1024]{1,0:T(8,128)(2,1)}), bf16[8192,1024]{1,0:T(8,128)(2,1)}) %all-gather.2.cloned.1.call-update) | async-done | bytes 16777232 | tf_op jit(solution)/shard_map/all_gather | solution.py:42
  160.0 12.9 %convolution_bitcast_fusion = f32[48,64,8,128]{3,2,1,0:T(8,128)} fusion(bf16[384,1024]{1,0:T(8,128)(2,1)S(1)} %copy-done.3, bf16[8192,1024]{1,0:T(8,128)(2,1)} %all-gather.2.cloned.1.call-done), kind=kOutput, calls=%fused_computation.24 | convolution fusion | flops 6442450944 | bytes 30146560 | tf_op jit(solution)/shard_map/dot_general | solution.py:45
  172.9 10.8 %copy.20 = f32[48,64,8,128]{3,2,0,1:T(8,128)} copy(f32[48,64,8,128]{3,2,1,0:T(8,128)} %convolution_bitcast_fusion) | data formatting | bytes 25165824 | tf_op jit(solution)/shard_map/reshape | solution.py:49
  183.7 8.7 %gather_fusion.1 = f32[40,384,128]{2,1,0:T(8,128)} fusion(f32[384,64,128]{2,0,1:T(8,128)} %bitcast.34, s32[1024]{0:T(1024)S(1)} %pad_clamp_fusion), kind=kCustom, calls=%fused_computation.1 | custom fusion | bytes 15728800 | tf_op jit(solution)/shard_map/jit(_take)/gather | solution.py:49
  192.4 9.1 %copy.16 = f32[384,40,128]{0,2,1:T(8,128)} copy(f32[384,40,128]{2,0,1:T(8,128)} %bitcast.35) | data formatting | bytes 15728640 | tf_op jit(solution)/shard_map/jit(_take)/gather | solution.py:49
  201.5 8.8 %fusion.10 = (f32[5120]{0:T(1024)S(1)}, f32[384]{0:T(512)S(1)}) fusion(bf16[384,5120]{0,1:T(8,128)(2,1)} %copy.12, f32[384,40,128]{0,2,1:T(8,128)} %copy.16, f32[384]{0:T(512)S(1)} %add_rsqrt_fusion, pred[5120]{0:T(1024)(128)(4,1)S(1)} %broadcast_bitcast_fusion.2, f32[5120]{0:T(1024)S(1)} %copy-done.4), kind=kLoop, calls=%fused_computation.19 | loop fusion | flops 15723136 | bytes 11845632 | tf_op jit(solution)/shard_map/reduce_sum | solution.py:65
  210.3 5.5 fusion.6
  215.8 6.3 %copy.13 = bf16[384,40,128]{2,0,1:T(8,128)(2,1)} copy(bf16[384,40,128]{0,2,1:T(8,128)(2,1)} %bitcast.37) | data formatting | bytes 7864320 | tf_op jit(solution)/shard_map/reshape | solution.py:38
  222.1 6.1 %gather_fusion = bf16[64,384,128]{2,1,0:T(8,128)(2,1)} fusion(bf16[384,40,128]{2,0,1:T(8,128)(2,1)} %copy.13, s32[1024]{0:T(1024)S(1)} %pad_clamp_fusion.1), kind=kCustom, calls=%fused_computation | custom fusion | bytes 12583168 | tf_op jit(solution)/shard_map/jit(_take)/gather | solution.py:39
  228.2 8.6 %copy.14 = bf16[384,64,128]{0,2,1:T(8,128)(2,1)} copy(bf16[384,64,128]{2,0,1:T(8,128)(2,1)} %bitcast.36) | data formatting | bytes 12582912 | tf_op jit(solution)/shard_map/jit(_take)/gather | solution.py:39
  236.8 6.9 %fusion.12 = bf16[384,8192]{0,1:T(8,128)(2,1)S(1)} fusion(bf16[384,64,128]{0,2,1:T(8,128)(2,1)} %copy.14, pred[8192]{0:T(1024)(128)(4,1)S(1)} %get-tuple-element.18, pred[8192]{0:T(1024)(128)(4,1)S(1)} %get-tuple-element.19), kind=kLoop, calls=%fused_computation.23 | loop fusion | flops 6291456 | bytes 12599296 | tf_op jit(solution)/shard_map/jit(_where)/select_n | solution.py:40
  243.7 2.6 copy-done.2
  246.3 11.7 %multiply_convert_fusion = bf16[8192,1024]{1,0:T(8,128)(2,1)} fusion(bf16[384,8192]{0,1:T(8,128)(2,1)S(1)} %fusion.12, bf16[384,1024]{1,0:T(8,128)(2,1)S(1)} %copy-done.3), kind=kOutput, calls=%fused_computation.3 | convolution fusion | flops 6459228160 | bytes 23855104 | tf_op jit(solution)/shard_map/dot_general | solution.py:56
  258.0 0.0 reduce-scatter.2.cloned.1.call-update
  258.0 0.0 copy-start.5
  258.0 0.1 convert_reduce_fusion
  258.2 6.3 %copy.17 = bf16[384,5120]{1,0:T(8,128)(2,1)} copy(bf16[384,5120]{0,1:T(8,128)(2,1)} %get-tuple-element.14) | data formatting | bytes 7864320
  264.4 42.3 %all-reduce = (f32[5120]{0:T(1024)}, f32[1024]{0:T(1024)}) all-reduce(f32[5120]{0:T(1024)S(1)} %broadcast_multiply_fusion, f32[1024]{0:T(1024)S(1)} %broadcast_multiply_fusion.1), channel_id=1, replica_groups=mesh['shard'=8,'rep'=4] {'shard','rep'}, use_global_device_ids=true, to_apply=%region_6.7 | all-reduce | flops 6144 | bytes 49152 | tf_op jit(solution)/shard_map/psum | solution.py:68
  306.7 13.0 %add_convert_fusion = bf16[384,1024]{1,0:T(8,128)(2,1)} fusion(bf16[384,8192]{0,1:T(8,128)(2,1)} %copy-done.2, bf16[8192,1024]{1,0:T(8,128)(2,1)} %all-gather.2.cloned.1.call-done, f32[1024]{0:T(1024)S(1)} %copy-done.5), kind=kOutput, calls=%fused_computation.26 | convolution fusion | flops 6443237376 | bytes 23859200 | tf_op jit(solution)/shard_map/dot_general | solution.py:44
  319.7 105.2 %reduce-scatter.2.cloned.1.call-done = bf16[1024,1024]{1,0:T(8,128)(2,1)} async-done(((bf16[8192,1024]{1,0:T(8,128)(2,1)}), bf16[1024,1024]{1,0:T(8,128)(2,1)}) %reduce-scatter.2.cloned.1.call-update) | async-done | bytes 2097168 | tf_op jit(solution)/shard_map/reduce_scatter | solution.py:54
  424.9 146.8 %all-reduce.2 = f32[1024,1024]{1,0:T(8,128)} all-reduce(bf16[1024,1024]{1,0:T(8,128)(2,1)} %reduce-scatter.2.cloned.1.call-done), channel_id=1, replica_groups=mesh['shard'=8,'rep'=4] {'rep'}, use_global_device_ids=true, to_apply=%region_4.5 | all-reduce | flops 1048576 | bytes 6291456 | tf_op jit(solution)/shard_map/psum | solution.py:67
  (20 shorter events, 0.1 us)
Async XLA Ops:
  7.2 7.1 %copy-start.6 = (s32[40]{0:T(128)S(1)}, s32[40]{0:T(128)}, u32[]{:S(2)}) copy-start(s32[40]{0:T(128)} %param.11) | copy-start | bytes 484
  7.2 152.8 %copy-start.3 = (bf16[384,1024]{1,0:T(8,128)(2,1)S(1)}, bf16[384,1024]{1,0:T(8,128)(2,1)}, u32[]{:S(2)}) copy-start(bf16[384,1024]{1,0:T(8,128)(2,1)} %param.10) | copy-start | bytes 2359300
  7.2 152.8 %all-gather.2.cloned.1.call-start = ((), (), s32[]{:S(2)}) async-start(), calls=%async_computation.1 | async-start | bytes 18874368 | tf_op jit(solution)/shard_map/all_gather | solution.py:42
  7.9 417.0 %reduce-scatter.2.cloned.1.call-start = ((), (), s32[]{:S(2)}) async-start(), calls=%async_computation.2 | async-start | bytes 18874368 | tf_op jit(solution)/shard_map/reduce_scatter | solution.py:54
  192.4 9.1 %copy-start.4 = (f32[5120]{0:T(1024)S(1)}, f32[5120]{0:T(1024)}, u32[]{:S(2)}) copy-start(f32[5120]{0:T(1024)} %param.7) | copy-start | bytes 61444
  201.5 8.8 %copy-start = (f32[384,40,128]{0,2,1:T(8,128)S(1)}, f32[384,40,128]{0,2,1:T(8,128)}, u32[]{:S(2)}) copy-start(f32[384,40,128]{0,2,1:T(8,128)} %copy.16) | copy-start | bytes 23592964
  201.5 8.8 %copy-start.1 = (bf16[384,5120]{0,1:T(8,128)(2,1)S(1)}, bf16[384,5120]{0,1:T(8,128)(2,1)}, u32[]{:S(2)}) copy-start(bf16[384,5120]{0,1:T(8,128)(2,1)} %copy.12) | copy-start | bytes 11796484
  243.7 2.6 copy-start.2
  258.0 48.7 %copy-start.5 = (f32[1024]{0:T(1024)S(1)}, f32[1024]{0:T(1024)}, u32[]{:S(2)}) copy-start(f32[1024]{0:T(1024)} %param.8) | copy-start | bytes 12292
Sparse Core Ops, SparseCore 0:
  9.6 150.3 all-gather.1
  258.1 166.7 reduce-scatter.1
where the time goes:
time: 580 us; the launch traced here: 579 us
  waiting for transfers between devices  248 us (43%)
  blocking collectives  189 us (33%)
  local copies, waits for them, and re-layouts  65.7 us (11%)
  matrix products  37.5 us (6%)
  other arithmetic  24.4 us (4%)
  between operations  14.2 us (2%)
    psum x1, blocking collectives, local(): weight_grad = lax.psum(group_sum, 'rep')  147 us
    all_gather x1, waiting for transfers between devices, local(): piece = lax.all_gather(key_weight, 'shard', axis=0, tiled=True)  142 us
    reduce_scatter x1, waiting for transfers between devices, local(): lax.psum_scatter((lax.dot_general(columns, cotangent, (((0,), (0,)), ((),...  105 us
    psum x1, blocking collectives, local(): gain_grad, bias_grad = lax.psum((gain_part, bias_part), ('shard', 'rep'))  42.3 us
    gather x2, local copies, waits for them, and re-layouts, local(): jnp.take(backward_part.reshape(row_count, slot_total, BLK), block_slot, a...  17.8 us
    unnamed x16, local copies, waits for them, and re-layouts  15.2 us
    gather x2, local copies, waits for them, and re-layouts, local(): jnp.take(normed_blocks, jnp.maximum(block_of_slot, 0), axis=1)  14.7 us
    dot_general x1, matrix products, local(): forward_sum = jnp.dot(columns, piece, preferred_element_type=jnp.float32)  13 us
  transfers between devices with their start and end apart: 2, of which 2 were waited for; matrix products, arithmetic and copies ran while one was open for 5% of the time, Pallas kernels for 0%

commit v1 on v0

--- a/solution.py
+++ b/solution.py
@@ -5,6 +5,11 @@
 
 BLK = 128
 EPS = 1e-06
+
+
+def add_all(shard, axis):
+    parts = lax.all_gather(shard, axis)
+    return jnp.sum(parts, axis=0)
 
 
 def normalize(tokens, norm_gain):
@@ -64,7 +69,7 @@
     ).astype(jnp.float32)
     gain_part = jnp.sum(grad_normed * values * inv_rms, axis=0) * grad_scale
     bias_part = jnp.sum(cotangent.astype(jnp.float32), axis=0) * grad_scale
-    weight_grad = lax.psum(group_sum, "rep")
+    weight_grad = add_all(group_sum, "rep")
     gain_grad, bias_grad = lax.psum((gain_part, bias_part), ("shard", "rep"))
     return (projected, token_grad, weight_grad, gain_grad, bias_grad)
 

time: 580 us -> 607 us (1.047)
  waiting for transfers between devices: 248 us -> 406 us
  blocking collectives: 189 us -> 42.2 us
  other arithmetic: 24.4 us -> 39 us
    psum x1 -> x0, blocking collectives: 147 us -> none  [local(): weight_grad = lax.psum(group_sum, 'rep')]
    all_gather x0 -> x1, waiting for transfers between devices: none -> 97.7 us  [add_all(): parts = lax.all_gather(shard, axis)]
    reduce_scatter x1, waiting for transfers between devices: 105 us -> 166 us  [local(): lax.psum_scatter((lax.dot_general(columns, cotangent, (((0,), (0,)), ((),...]
    reduce_sum x0 -> x1, other arithmetic: none -> 10.4 us  [add_all(): return jnp.sum(parts, axis=0)]
  transfers between devices with their start and end apart: 2 -> 3, of which waited for: 2 -> 3; matrix products, arithmetic and copies ran while one was open for 5% -> 5% of each run, Pallas kernels for 0% -> 0%
where the time goes in v1:
time: 607 us; the launch traced here: 604 us
  waiting for transfers between devices  406 us (67%)
  local copies, waits for them, and re-layouts  65.8 us (11%)
  blocking collectives  42.2 us (7%)
  other arithmetic  39 us (6%)
  matrix products  37.4 us (6%)
  between operations  13.9 us (2%)
    reduce_scatter x1, waiting for transfers between devices, local(): lax.psum_scatter((lax.dot_general(columns, cotangent, (((0,), (0,)), ((),...  166 us
    all_gather x1, waiting for transfers between devices, local(): piece = lax.all_gather(key_weight, 'shard', axis=0, tiled=True)  142 us
    all_gather x1, waiting for transfers between devices, add_all(): parts = lax.all_gather(shard, axis)  97.7 us
    psum x1, blocking collectives, local(): gain_grad, bias_grad = lax.psum((gain_part, bias_part), ('shard', 'rep'))  42.2 us
    gather x2, local copies, waits for them, and re-layouts, local(): jnp.take(backward_part.reshape(row_count, slot_total, BLK), block_slot, a...  17.8 us
    unnamed x16, local copies, waits for them, and re-layouts  15.3 us
    gather x2, local copies, waits for them, and re-layouts, local(): jnp.take(normed_blocks, jnp.maximum(block_of_slot, 0), axis=1)  14.7 us
    dot_general x1, matrix products, local(): forward_sum = jnp.dot(columns, piece, preferred_element_type=jnp.float32)  12.9 us
  transfers between devices with their start and end apart: 3, of which 3 were waited for; matrix products, arithmetic and copies ran while one was open for 5% of the time, Pallas kernels for 0%

profile of v1, /device:TPU:16, one launch (start us, length us, event | category | flops | bytes accessed | tf_op | source)
XLA Modules:
  0.0 604.4 jit_solution(3807886448294225196)
XLA Ops:
  7.2 0.0 all-gather.4.cloned.1.call-start
  7.2 0.7 all-gather.4.cloned.1.call-update
  7.9 0.0 reduce-scatter.2.cloned.1.call-start
  8.0 6.3 %copy.12 = bf16[384,5120]{0,1:T(8,128)(2,1)} copy(bf16[384,5120]{1,0:T(8,128)(2,1)} %param.6) | data formatting | bytes 7864320 | tf_op args[0]
  14.2 0.7 scatter_custom_fusion
  15.0 3.0 fusion.7
  18.1 0.1 broadcast_bitcast_fusion.2
  18.1 0.1 broadcast_bitcast_fusion
  18.2 141.7 %all-gather.4.cloned.1.call-done = bf16[8192,1024]{1,0:T(8,128)(2,1)} async-done(((bf16[1024,1024]{1,0:T(8,128)(2,1)}), bf16[8192,1024]{1,0:T(8,128)(2,1)}) %all-gather.4.cloned.1.call-update) | async-done | bytes 16777232 | tf_op jit(solution)/shard_map/all_gather | solution.py:47
  160.0 12.9 %convolution_bitcast_fusion = f32[48,64,8,128]{3,2,1,0:T(8,128)} fusion(bf16[384,1024]{1,0:T(8,128)(2,1)S(1)} %copy-done.3, bf16[8192,1024]{1,0:T(8,128)(2,1)} %all-gather.4.cloned.1.call-done), kind=kOutput, calls=%fused_computation.24 | convolution fusion | flops 6442450944 | bytes 30146560 | tf_op jit(solution)/shard_map/dot_general | solution.py:50
  172.9 10.8 %copy.20 = f32[48,64,8,128]{3,2,0,1:T(8,128)} copy(f32[48,64,8,128]{3,2,1,0:T(8,128)} %convolution_bitcast_fusion) | data formatting | bytes 25165824 | tf_op jit(solution)/shard_map/reshape | solution.py:54
  183.7 8.7 %gather_fusion.1 = f32[40,384,128]{2,1,0:T(8,128)} fusion(f32[384,64,128]{2,0,1:T(8,128)} %bitcast.35, s32[1024]{0:T(1024)S(1)} %pad_clamp_fusion), kind=kCustom, calls=%fused_computation.1 | custom fusion | bytes 15728800 | tf_op jit(solution)/shard_map/jit(_take)/gather | solution.py:54
  192.4 9.1 %copy.16 = f32[384,40,128]{0,2,1:T(8,128)} copy(f32[384,40,128]{2,0,1:T(8,128)} %bitcast.36) | data formatting | bytes 15728640 | tf_op jit(solution)/shard_map/jit(_take)/gather | solution.py:54
  201.5 8.8 %fusion.10 = (f32[5120]{0:T(1024)S(1)}, f32[384]{0:T(512)S(1)}) fusion(bf16[384,5120]{0,1:T(8,128)(2,1)} %copy.12, f32[384,40,128]{0,2,1:T(8,128)} %copy.16, f32[384]{0:T(512)S(1)} %add_rsqrt_fusion, pred[5120]{0:T(1024)(128)(4,1)S(1)} %broadcast_bitcast_fusion.2, f32[5120]{0:T(1024)S(1)} %copy-done.4), kind=kLoop, calls=%fused_computation.19 | loop fusion | flops 15723136 | bytes 11845632 | tf_op jit(solution)/shard_map/reduce_sum | solution.py:70
  210.3 5.6 fusion.6
  216.0 6.3 %copy.13 = bf16[384,40,128]{2,0,1:T(8,128)(2,1)} copy(bf16[384,40,128]{0,2,1:T(8,128)(2,1)} %bitcast.39) | data formatting | bytes 7864320 | tf_op jit(solution)/shard_map/reshape | solution.py:43
  222.2 6.1 %gather_fusion = bf16[64,384,128]{2,1,0:T(8,128)(2,1)} fusion(bf16[384,40,128]{2,0,1:T(8,128)(2,1)} %copy.13, s32[1024]{0:T(1024)S(1)} %pad_clamp_fusion.1), kind=kCustom, calls=%fused_computation | custom fusion | bytes 12583168 | tf_op jit(solution)/shard_map/jit(_take)/gather | solution.py:44
  228.3 8.6 %copy.14 = bf16[384,64,128]{0,2,1:T(8,128)(2,1)} copy(bf16[384,64,128]{2,0,1:T(8,128)(2,1)} %bitcast.37) | data formatting | bytes 12582912 | tf_op jit(solution)/shard_map/jit(_take)/gather | solution.py:44
  237.0 6.9 %fusion.12 = bf16[384,8192]{0,1:T(8,128)(2,1)S(1)} fusion(bf16[384,64,128]{0,2,1:T(8,128)(2,1)} %copy.14, pred[8192]{0:T(1024)(128)(4,1)S(1)} %get-tuple-element.18, pred[8192]{0:T(1024)(128)(4,1)S(1)} %get-tuple-element.19), kind=kLoop, calls=%fused_computation.23 | loop fusion | flops 6291456 | bytes 12599296 | tf_op jit(solution)/shard_map/jit(_where)/select_n | solution.py:45
  243.9 2.6 copy-done.2
  246.5 11.7 %multiply_convert_fusion = bf16[8192,1024]{1,0:T(8,128)(2,1)} fusion(bf16[384,8192]{0,1:T(8,128)(2,1)S(1)} %fusion.12, bf16[384,1024]{1,0:T(8,128)(2,1)S(1)} %copy-done.3), kind=kOutput, calls=%fused_computation.3 | convolution fusion | flops 6459228160 | bytes 23855104 | tf_op jit(solution)/shard_map/dot_general | solution.py:61
  258.1 0.0 reduce-scatter.2.cloned.1.call-update
  258.1 0.0 all-gather.6.cloned.1.call-start
  258.2 165.8 %reduce-scatter.2.cloned.1.call-done = bf16[1024,1024]{1,0:T(8,128)(2,1)} async-done(((bf16[8192,1024]{1,0:T(8,128)(2,1)}), bf16[1024,1024]{1,0:T(8,128)(2,1)}) %reduce-scatter.2.cloned.1.call-update) | async-done | bytes 2097168 | tf_op jit(solution)/shard_map/reduce_scatter | solution.py:59
  424.0 4.1 all_gather.16
  428.1 0.0 all-gather.6.cloned.1.call-update
  428.1 0.1 convert_reduce_fusion
  428.2 6.5 %copy.17 = bf16[384,5120]{1,0:T(8,128)(2,1)} copy(bf16[384,5120]{0,1:T(8,128)(2,1)} %get-tuple-element.14) | data formatting | bytes 7864320
  434.7 42.2 %all-reduce = (f32[5120]{0:T(1024)}, f32[1024]{0:T(1024)}) all-reduce(f32[5120]{0:T(1024)S(1)} %broadcast_multiply_fusion, f32[1024]{0:T(1024)S(1)} %broadcast_multiply_fusion.1), channel_id=1, replica_groups=mesh['shard'=8,'rep'=4] {'shard','rep'}, use_global_device_ids=true, to_apply=%region_6.7 | all-reduce | flops 6144 | bytes 49152 | tf_op jit(solution)/shard_map/psum | solution.py:73
  476.9 12.9 %add_convert_fusion = bf16[384,1024]{1,0:T(8,128)(2,1)} fusion(bf16[384,8192]{0,1:T(8,128)(2,1)} %copy-done.2, bf16[8192,1024]{1,0:T(8,128)(2,1)} %all-gather.4.cloned.1.call-done, f32[1024]{0:T(1024)S(1)} %copy-done.5), kind=kOutput, calls=%fused_computation.26 | convolution fusion | flops 6443237376 | bytes 23859200 | tf_op jit(solution)/shard_map/dot_general | solution.py:49
  489.8 97.7 %all-gather.6.cloned.1.call-done = f32[4096,1024]{1,0:T(8,128)} async-done(((f32[1024,1024]{1,0:T(8,128)}), f32[4096,1024]{1,0:T(8,128)}) %all-gather.6.cloned.1.call-update) | async-done | bytes 16777232 | tf_op jit(solution)/shard_map/all_gather | solution.py:11
  587.5 10.4 %reduce_sum.47 = f32[1024,1024]{1,0:T(8,128)} reduce(f32[4,1024,1024]{2,1,0:T(8,128)} %bitcast.38, f32[]{:T(128)} %constant.26.clone.1), dimensions={0}, to_apply=%region_4.5 | reduce | flops 3145728 | bytes 20971524 | tf_op jit(solution)/shard_map/reduce_sum | solution.py:12
  (24 shorter events, 0.1 us)
Async XLA Ops:
  7.2 7.1 %copy-start.6 = (s32[40]{0:T(128)S(1)}, s32[40]{0:T(128)}, u32[]{:S(2)}) copy-start(s32[40]{0:T(128)} %param.11) | copy-start | bytes 484
  7.2 152.8 %copy-start.3 = (bf16[384,1024]{1,0:T(8,128)(2,1)S(1)}, bf16[384,1024]{1,0:T(8,128)(2,1)}, u32[]{:S(2)}) copy-start(bf16[384,1024]{1,0:T(8,128)(2,1)} %param.10) | copy-start | bytes 2359300
  7.2 152.8 %all-gather.4.cloned.1.call-start = ((), (), s32[]{:S(2)}) async-start(), calls=%async_computation.1 | async-start | bytes 18874368 | tf_op jit(solution)/shard_map/all_gather | solution.py:47
  7.9 416.1 %reduce-scatter.2.cloned.1.call-start = ((), (), s32[]{:S(2)}) async-start(), calls=%async_computation.2 | async-start | bytes 18874368 | tf_op jit(solution)/shard_map/reduce_scatter | solution.py:59
  192.4 9.1 %copy-start.4 = (f32[5120]{0:T(1024)S(1)}, f32[5120]{0:T(1024)}, u32[]{:S(2)}) copy-start(f32[5120]{0:T(1024)} %param.7) | copy-start | bytes 61444
  201.5 8.8 %copy-start = (f32[384,40,128]{0,2,1:T(8,128)S(1)}, f32[384,40,128]{0,2,1:T(8,128)}, u32[]{:S(2)}) copy-start(f32[384,40,128]{0,2,1:T(8,128)} %copy.16) | copy-start | bytes 23592964
  201.5 8.8 %copy-start.1 = (bf16[384,5120]{0,1:T(8,128)(2,1)S(1)}, bf16[384,5120]{0,1:T(8,128)(2,1)}, u32[]{:S(2)}) copy-start(bf16[384,5120]{0,1:T(8,128)(2,1)} %copy.12) | copy-start | bytes 11796484
  243.9 2.6 copy-start.2
  258.1 329.3 %all-gather.6.cloned.1.call-start = ((), (), s32[]{:S(2)}) async-start(), calls=%async_computation.3 | async-start | bytes 20971520 | tf_op jit(solution)/shard_map/all_gather | solution.py:11
  428.1 48.8 %copy-start.5 = (f32[1024]{0:T(1024)S(1)}, f32[1024]{0:T(1024)}, u32[]{:S(2)}) copy-start(f32[1024]{0:T(1024)} %param.8) | copy-start | bytes 12292
Sparse Core Ops, SparseCore 0:
  9.6 150.3 all-gather.3
  258.3 165.6 reduce-scatter.1
  428.2 159.2 all-gather.5
